TPU v7x, 32 devices: a whole 2x2x4 slice. The times are simulated.
32 devices in a mesh: wide: 8 (over y, x, core), narrow: 4 (over z).
Axes of the slice: x: 2, y: 2, z: 4, core: 2. Of those that a mesh axis runs over, the one named last changes fastest.
Arguments:
- image: bfloat16 [2, 256, 256, 256], P(None, 'wide', 'narrow'), may hold values from -6 to 6
- deapodization: float32 [3, 256], replicated, may hold values from 0.5 to 2
- offsets: int32 [32, 8], P(('wide', 'narrow')), may hold values from 0 to 256
- cross_weight: bfloat16 [32, 8, 1536, 1024], P(('wide', 'narrow')), may hold values from -0.1875 to 0.1875
- x_weight: bfloat16 [32, 8, 1536, 256], P(('wide', 'narrow')), may hold values from -0.375 to 0.375
Outputs:
- samples: float32 [32, 8, 2, 1536], P(('wide', 'narrow'))
Inputs may be any that keep to these rules, and one draw needn't show every extreme that they name: `offsets`: each entry is the first row, along the first frequency dimension, of a group's window of 256 rows in one slab.
All inputs are finite; a program needn't handle non-finite values.
Results may differ from a plain program's by a relative error of at most 0.007.
Values may be sent and summed in bfloat16 or wider, within the bound.
A program may use at most 128 MiB of HBM per device.

v0:
```python
import math
import jax
import jax.numpy as jnp
from jax import lax
from jax.sharding import PartitionSpec as P

G = 512
KZ = 64
BX = 256
SAMP = 1536


def shifted(block, axis, distance):
    devices = range(lax.axis_size(axis))
    route = [((i - distance) % len(devices), i) for i in devices]
    return lax.ppermute(block, axis, route)


def block_table(out_rows, inputs, grid_size, lowest):
    frequency = jnp.arange(out_rows, dtype=jnp.int32) + lowest
    position = jnp.arange(inputs, dtype=jnp.int32) - inputs // 2
    phases = jnp.mod(frequency[:, None] * position[None, :], grid_size)
    angles = phases.astype(jnp.float32) * (2.0 * math.pi / grid_size)
    factor = 1.0 / math.sqrt(inputs)
    cosine = (jnp.cos(angles) * factor).astype(jnp.bfloat16)
    sine = (jnp.sin(angles) * factor).astype(jnp.bfloat16)
    real_rows = jnp.stack([cosine, sine], axis=1)
    imag_rows = jnp.stack([-sine, cosine], axis=1)
    return jnp.stack([real_rows, imag_rows], axis=0)


def window_samples(window_rows, cross_rows, window_gain):
    partial_value = jnp.einsum(
        "ms,qcs->cmq", cross_rows, window_rows, preferred_element_type=jnp.float32
    )
    return jnp.sum(partial_value * window_gain.astype(jnp.float32)[None], axis=-1)


def per_device(image, deapodization, offsets, cross_weight, x_weight):
    wide_count = lax.axis_size("wide")
    wide_index = lax.axis_index("wide")
    narrow_index = lax.axis_index("narrow")
    block_x = image.shape[1]
    block_y = image.shape[2]
    image_width = image.shape[3]
    scale_x = lax.dynamic_slice_in_dim(deapodization[0], wide_index * block_x, block_x)
    scale_y = lax.dynamic_slice_in_dim(deapodization[1], narrow_index * block_y, block_y)
    weighted = (
        image.astype(jnp.float32)
        * scale_x[None, :, None, None]
        * scale_y[None, None, :, None]
        * deapodization[2][None, None, None, :]
    ).astype(jnp.bfloat16)
    z_table = block_table(KZ, image_width, G, -(KZ // 2))
    band_data = (
        jnp.einsum("okcz,cxyz->xyko", z_table, weighted, preferred_element_type=jnp.float32)
        .astype(jnp.bfloat16)
        .reshape(block_x, block_y, 2 * KZ)
    )
    line_table = block_table(G, image_width, G, -(G // 2))
    pieces = lax.all_to_all(band_data, "narrow", split_axis=2, concat_axis=1, tiled=True)
    item_count = pieces.shape[0]
    band_depth = pieces.shape[2] // 2
    unpacked = pieces.reshape(item_count, image_width, band_depth, 2)
    product = jnp.einsum(
        "oqcy,xykc->xoqk", line_table, unpacked, preferred_element_type=jnp.float32
    )
    columns = product.astype(jnp.bfloat16).reshape(item_count, 2, G * band_depth)
    slab_lines = lax.all_to_all(columns, "wide", split_axis=2, concat_axis=0, tiled=True)

    def transform_rows(table_rows, source):
        product = jnp.einsum(
            "opcx,xcs->pos", table_rows, source, preferred_element_type=jnp.float32
        )
        return product.astype(jnp.bfloat16)

    def slab_samples(slab_data, slab_index):
        start_row = lax.dynamic_index_in_dim(offsets[0], slab_index, 0, False)
        cross_rows = lax.dynamic_index_in_dim(cross_weight[0], slab_index, 0, False)
        window_gain = lax.dynamic_index_in_dim(x_weight[0], slab_index, 0, False)
        part_table = block_table(BX, image_width, G, start_row - G // 2)
        window_rows = transform_rows(part_table, slab_data)
        return window_samples(window_rows, cross_rows, window_gain)

    def record(results, slab_data, slab_index):
        return lax.dynamic_update_index_in_dim(
            results, slab_samples(slab_data, slab_index), slab_index, 0
        )

    results = jnp.zeros((wide_count, 2, SAMP), jnp.float32)

    def one_hop(hop_count, carried):
        current, results = carried
        incoming = shifted(current, "wide", 1)
        results = record(results, current, jnp.mod(wide_index - hop_count, wide_count))
        return (incoming, results)

    current, results = lax.fori_loop(0, wide_count - 1, one_hop, (slab_lines, results))
    results = record(results, current, jnp.mod(wide_index - (wide_count - 1), wide_count))
    return results[None]


def solution(mesh):
    return jax.shard_map(
        per_device,
        mesh=mesh,
        in_specs=(
            P(None, "wide", "narrow", None),
            P(),
            P(("wide", "narrow"), None),
            P(("wide", "narrow"), None, None, None),
            P(("wide", "narrow"), None, None, None),
        ),
        out_specs=P(("wide", "narrow"), None, None, None),
        check_vma=False,
    )
```

profile of v0, /device:TPU:0, one launch (start us, length us, event | category | flops | bytes accessed | tf_op | source)
XLA Modules:
  0.0 221.7 jit_solution(11140627748605231871)
XLA Ops:
  9.3 6.3 %all-to-all-start = ((bf16[4,2,32768]{2,1,0:T(2,128)(2,1)}), bf16[4,2,32768]{2,1,0:T(2,128)(2,1)S(1)}, u32[]{:S(2)}, u32[]{:S(2)}) async-start(bf16[4,2,32768]{2,1,0:T(2,128)(2,1)} %reshape.794), calls=%async_computation | async-start | bytes 1048576 | tf_op jit(solution)/shard_map/all_to_all | solution.py:61
  20.5 9.6 %all-to-all-done = bf16[4,2,32768]{2,1,0:T(2,128)(2,1)S(1)} async-done(((bf16[4,2,32768]{2,1,0:T(2,128)(2,1)}), bf16[4,2,32768]{2,1,0:T(2,128)(2,1)S(1)}, u32[]{:S(2)}, u32[]{:S(2)}) %all-to-all-start) | async-done | bytes 524320 | tf_op jit(solution)/shard_map/all_to_all | solution.py:61
  35.0 5.1 %copy.35 = bf16[32,2,512,16]{0,3,2,1:T(8,128)(2,1)} copy(bf16[32,2,512,16]{2,3,1,0:T(8,128)(2,1)S(1)} %fusion.37) | data formatting | bytes 2097152 | tf_op jit(solution)/shard_map/convert_element_type | solution.py:68
  40.0 10.1 %copy.69 = bf16[32,2,8192]{0,1,2:T(2,128)(2,1)} copy(bf16[32,2,8192]{0,2,1:T(8,128)(2,1)} %bitcast.154) | data formatting | bytes 2097152 | tf_op jit(solution)/shard_map/reshape | solution.py:68
  50.1 7.8 %reshape.796 = bf16[8,2,32768]{2,1,0:T(2,128)(2,1)} reshape(bf16[8192,2,32]{2,1,0:T(2,128)(2,1)} %bitcast.155) | data formatting | bytes 2097152
  67.0 10.0 %all-to-all-done.1 = bf16[8,2,32768]{2,1,0:T(2,128)(2,1)S(1)} async-done(((bf16[8,2,32768]{2,1,0:T(2,128)(2,1)}), bf16[8,2,32768]{2,1,0:T(2,128)(2,1)S(1)}, u32[]{:S(2)}, u32[]{:S(2)}) %all-to-all-start.1) | async-done | bytes 1048608 | tf_op jit(solution)/shard_map/all_to_all | solution.py:69
  77.0 4.5 %reshape.797 = bf16[8192,2,32]{2,1,0:T(2,128)(2,1)} reshape(bf16[8,2,32768]{2,1,0:T(2,128)(2,1)S(1)} %all-to-all-done.1) | data formatting | bytes 2097152
  81.6 10.4 %copy.57 = bf16[32,2,8,1024]{3,0,2,1:T(8,128)(2,1)} copy(bf16[32,2,8,1024]{0,1,3,2:T(2,128)(2,1)} %bitcast.153) | data formatting | bytes 2097152 | tf_op jit(solution)/shard_map/all_to_all | solution.py:69
  92.0 123.9 %while.18 = (s32[]{:T(128)}, bf16[256,2,1024]{2,0,1:T(8,128)(2,1)}, f32[8,2,1536]{2,1,0:T(2,128)S(1)}, s32[]{:T(128)}, s32[1,8]{1,0:T(1,128)S(1)}, /*index=5*/bf...) while((s32[]{:T(128)}, bf16[256,2,1024]{2,0,1:T(8,128)(2,1)}, ...), condition=%wide.region_2.3_spmd, body=%wide.region_0.2_spmd.sunk | while | flops 2152920576 | bytes 19441996 | solution.py:98
  99.6 4.6 %fusion.88 = f32[2,1536]{1,0:T(2,128)S(1)} fusion(f32[1536,256]{0,1:T(8,128)S(1)} %bitcast_convert_fusion.7, bf16[1,8,1536,1024]{3,2,1,0:T(8,128)(2,1)} %get-tuple-element.363, s32[]{:T(128)S(6)} %select_n.233, bf16[256,2,1024]{2,0,1:T(8,128)(2,1)} %copy.77, bf16[1,256,2,256]{3,1,2,0:T(8,128)(2,1)S(1)} %get-tuple-element.334, ...), kind=kOutput, calls=%fused_computation.5.clone.1 | convolution fusion | flops 2149839872 | bytes 6303748 | tf_op jit(solution)/shard_map/while/body/eval_jaxpr/ms,qcs->cmq/dot_general | solution.py:33
  104.2 5.5 %collective-permute-done = bf16[256,2,1024]{2,0,1:T(8,128)(2,1)} collective-permute-done((bf16[256,2,1024]{2,0,1:T(8,128)(2,1)}, bf16[256,2,1024]{2,0,1:T(8,128)(2,1)}, u32[]{:S(2)}, u32[]{:S(2)}) %collective-permute-start) | collective-permute-done | bytes 1048608 | tf_op jit(solution)/shard_map/while/body/eval_jaxpr/ppermute | solution.py:16
  117.3 4.6 %fusion.88 = f32[2,1536]{1,0:T(2,128)S(1)} fusion(f32[1536,256]{0,1:T(8,128)S(1)} %bitcast_convert_fusion.7, bf16[1,8,1536,1024]{3,2,1,0:T(8,128)(2,1)} %get-tuple-element.363, s32[]{:T(128)S(6)} %select_n.233, bf16[256,2,1024]{2,0,1:T(8,128)(2,1)} %copy.77, bf16[1,256,2,256]{3,1,2,0:T(8,128)(2,1)S(1)} %get-tuple-element.334, ...), kind=kOutput, calls=%fused_computation.5.clone.1 | convolution fusion | flops 2149839872 | bytes 6303748 | tf_op jit(solution)/shard_map/while/body/eval_jaxpr/ms,qcs->cmq/dot_general | solution.py:33
  121.9 5.5 %collective-permute-done = bf16[256,2,1024]{2,0,1:T(8,128)(2,1)} collective-permute-done((bf16[256,2,1024]{2,0,1:T(8,128)(2,1)}, bf16[256,2,1024]{2,0,1:T(8,128)(2,1)}, u32[]{:S(2)}, u32[]{:S(2)}) %collective-permute-start) | collective-permute-done | bytes 1048608 | tf_op jit(solution)/shard_map/while/body/eval_jaxpr/ppermute | solution.py:16
  135.0 4.6 %fusion.88 = f32[2,1536]{1,0:T(2,128)S(1)} fusion(f32[1536,256]{0,1:T(8,128)S(1)} %bitcast_convert_fusion.7, bf16[1,8,1536,1024]{3,2,1,0:T(8,128)(2,1)} %get-tuple-element.363, s32[]{:T(128)S(6)} %select_n.233, bf16[256,2,1024]{2,0,1:T(8,128)(2,1)} %copy.77, bf16[1,256,2,256]{3,1,2,0:T(8,128)(2,1)S(1)} %get-tuple-element.334, ...), kind=kOutput, calls=%fused_computation.5.clone.1 | convolution fusion | flops 2149839872 | bytes 6303748 | tf_op jit(solution)/shard_map/while/body/eval_jaxpr/ms,qcs->cmq/dot_general | solution.py:33
  139.6 5.5 %collective-permute-done = bf16[256,2,1024]{2,0,1:T(8,128)(2,1)} collective-permute-done((bf16[256,2,1024]{2,0,1:T(8,128)(2,1)}, bf16[256,2,1024]{2,0,1:T(8,128)(2,1)}, u32[]{:S(2)}, u32[]{:S(2)}) %collective-permute-start) | collective-permute-done | bytes 1048608 | tf_op jit(solution)/shard_map/while/body/eval_jaxpr/ppermute | solution.py:16
  152.7 4.6 %fusion.88 = f32[2,1536]{1,0:T(2,128)S(1)} fusion(f32[1536,256]{0,1:T(8,128)S(1)} %bitcast_convert_fusion.7, bf16[1,8,1536,1024]{3,2,1,0:T(8,128)(2,1)} %get-tuple-element.363, s32[]{:T(128)S(6)} %select_n.233, bf16[256,2,1024]{2,0,1:T(8,128)(2,1)} %copy.77, bf16[1,256,2,256]{3,1,2,0:T(8,128)(2,1)S(1)} %get-tuple-element.334, ...), kind=kOutput, calls=%fused_computation.5.clone.1 | convolution fusion | flops 2149839872 | bytes 6303748 | tf_op jit(solution)/shard_map/while/body/eval_jaxpr/ms,qcs->cmq/dot_general | solution.py:33
  157.3 5.5 %collective-permute-done = bf16[256,2,1024]{2,0,1:T(8,128)(2,1)} collective-permute-done((bf16[256,2,1024]{2,0,1:T(8,128)(2,1)}, bf16[256,2,1024]{2,0,1:T(8,128)(2,1)}, u32[]{:S(2)}, u32[]{:S(2)}) %collective-permute-start) | collective-permute-done | bytes 1048608 | tf_op jit(solution)/shard_map/while/body/eval_jaxpr/ppermute | solution.py:16
  170.4 4.6 %fusion.88 = f32[2,1536]{1,0:T(2,128)S(1)} fusion(f32[1536,256]{0,1:T(8,128)S(1)} %bitcast_convert_fusion.7, bf16[1,8,1536,1024]{3,2,1,0:T(8,128)(2,1)} %get-tuple-element.363, s32[]{:T(128)S(6)} %select_n.233, bf16[256,2,1024]{2,0,1:T(8,128)(2,1)} %copy.77, bf16[1,256,2,256]{3,1,2,0:T(8,128)(2,1)S(1)} %get-tuple-element.334, ...), kind=kOutput, calls=%fused_computation.5.clone.1 | convolution fusion | flops 2149839872 | bytes 6303748 | tf_op jit(solution)/shard_map/while/body/eval_jaxpr/ms,qcs->cmq/dot_general | solution.py:33
  175.0 5.5 %collective-permute-done = bf16[256,2,1024]{2,0,1:T(8,128)(2,1)} collective-permute-done((bf16[256,2,1024]{2,0,1:T(8,128)(2,1)}, bf16[256,2,1024]{2,0,1:T(8,128)(2,1)}, u32[]{:S(2)}, u32[]{:S(2)}) %collective-permute-start) | collective-permute-done | bytes 1048608 | tf_op jit(solution)/shard_map/while/body/eval_jaxpr/ppermute | solution.py:16
  188.1 4.6 %fusion.88 = f32[2,1536]{1,0:T(2,128)S(1)} fusion(f32[1536,256]{0,1:T(8,128)S(1)} %bitcast_convert_fusion.7, bf16[1,8,1536,1024]{3,2,1,0:T(8,128)(2,1)} %get-tuple-element.363, s32[]{:T(128)S(6)} %select_n.233, bf16[256,2,1024]{2,0,1:T(8,128)(2,1)} %copy.77, bf16[1,256,2,256]{3,1,2,0:T(8,128)(2,1)S(1)} %get-tuple-element.334, ...), kind=kOutput, calls=%fused_computation.5.clone.1 | convolution fusion | flops 2149839872 | bytes 6303748 | tf_op jit(solution)/shard_map/while/body/eval_jaxpr/ms,qcs->cmq/dot_general | solution.py:33
  192.7 5.5 %collective-permute-done = bf16[256,2,1024]{2,0,1:T(8,128)(2,1)} collective-permute-done((bf16[256,2,1024]{2,0,1:T(8,128)(2,1)}, bf16[256,2,1024]{2,0,1:T(8,128)(2,1)}, u32[]{:S(2)}, u32[]{:S(2)}) %collective-permute-start) | collective-permute-done | bytes 1048608 | tf_op jit(solution)/shard_map/while/body/eval_jaxpr/ppermute | solution.py:16
  205.8 4.6 %fusion.88 = f32[2,1536]{1,0:T(2,128)S(1)} fusion(f32[1536,256]{0,1:T(8,128)S(1)} %bitcast_convert_fusion.7, bf16[1,8,1536,1024]{3,2,1,0:T(8,128)(2,1)} %get-tuple-element.363, s32[]{:T(128)S(6)} %select_n.233, bf16[256,2,1024]{2,0,1:T(8,128)(2,1)} %copy.77, bf16[1,256,2,256]{3,1,2,0:T(8,128)(2,1)S(1)} %get-tuple-element.334, ...), kind=kOutput, calls=%fused_computation.5.clone.1 | convolution fusion | flops 2149839872 | bytes 6303748 | tf_op jit(solution)/shard_map/while/body/eval_jaxpr/ms,qcs->cmq/dot_general | solution.py:33
  210.4 5.5 %collective-permute-done = bf16[256,2,1024]{2,0,1:T(8,128)(2,1)} collective-permute-done((bf16[256,2,1024]{2,0,1:T(8,128)(2,1)}, bf16[256,2,1024]{2,0,1:T(8,128)(2,1)}, u32[]{:S(2)}, u32[]{:S(2)}) %collective-permute-start) | collective-permute-done | bytes 1048608 | tf_op jit(solution)/shard_map/while/body/eval_jaxpr/ppermute | solution.py:16
  215.9 5.1 %fusion.29 = f32[2,1536]{1,0:T(2,128)S(1)} fusion(f32[1536,256]{0,1:T(8,128)} %copy.42, bf16[1,8,1536,1024]{3,2,1,0:T(8,128)(2,1)} %get-tuple-element.371, s32[]{:T(128)S(6)} %select_n.180, bf16[256,2,1024]{2,0,1:T(8,128)(2,1)} %get-tuple-element.215, bf16[1,256,2,256]{3,1,2,0:T(8,128)(2,1)S(1)} %get-tuple-element.267, ...), kind=kOutput, calls=%fused_computation.43 | convolution fusion | flops 2150626304 | bytes 6303748 | tf_op jit(solution)/shard_map/ms,qcs->cmq/dot_general | solution.py:33
  (109 shorter events, 81.5 us)
Async XLA Ops:
  9.3 20.8 %all-to-all-start = ((bf16[4,2,32768]{2,1,0:T(2,128)(2,1)}), bf16[4,2,32768]{2,1,0:T(2,128)(2,1)S(1)}, u32[]{:S(2)}, u32[]{:S(2)}) async-start(bf16[4,2,32768]{2,1,0:T(2,128)(2,1)} %reshape.794), calls=%async_computation | async-start | bytes 1048576 | tf_op jit(solution)/shard_map/all_to_all | solution.py:61
  57.9 19.1 %all-to-all-start.1 = ((bf16[8,2,32768]{2,1,0:T(2,128)(2,1)}), bf16[8,2,32768]{2,1,0:T(2,128)(2,1)S(1)}, u32[]{:S(2)}, u32[]{:S(2)}) async-start(bf16[8,2,32768]{2,1,0:T(2,128)(2,1)} %reshape.796), calls=%async_computation.1 | async-start | bytes 2097152 | tf_op jit(solution)/shard_map/all_to_all | solution.py:69
  81.5 10.4 %copy-start.1 = (s32[1,8]{1,0:T(1,128)S(1)}, s32[1,8]{1,0:T(1,128)}, u32[]{:S(2)}) copy-start(s32[1,8]{1,0:T(1,128)} %param.9) | copy-start | bytes 100
  94.3 15.4 %collective-permute-start = (bf16[256,2,1024]{2,0,1:T(8,128)(2,1)}, bf16[256,2,1024]{2,0,1:T(8,128)(2,1)}, u32[]{:S(2)}, u32[]{:S(2)}) collective-permute-start(bf16[256,2,1024]{2,0,1:T(8,128)(2,1)} %copy.77), channel_id=1, source_target_pairs={{28,0},{0,4},{4,8},{8,12},{12,16},{16,20},{20,24},{24,28},{29,1},{... | collective-permute-start | bytes 3145736 | tf_op jit(solution)/shard_map/while/body/eval_jaxpr/ppermute | solution.py:16
  112.0 15.4 %collective-permute-start = (bf16[256,2,1024]{2,0,1:T(8,128)(2,1)}, bf16[256,2,1024]{2,0,1:T(8,128)(2,1)}, u32[]{:S(2)}, u32[]{:S(2)}) collective-permute-start(bf16[256,2,1024]{2,0,1:T(8,128)(2,1)} %copy.77), channel_id=1, source_target_pairs={{28,0},{0,4},{4,8},{8,12},{12,16},{16,20},{20,24},{24,28},{29,1},{... | collective-permute-start | bytes 3145736 | tf_op jit(solution)/shard_map/while/body/eval_jaxpr/ppermute | solution.py:16
  129.7 15.4 %collective-permute-start = (bf16[256,2,1024]{2,0,1:T(8,128)(2,1)}, bf16[256,2,1024]{2,0,1:T(8,128)(2,1)}, u32[]{:S(2)}, u32[]{:S(2)}) collective-permute-start(bf16[256,2,1024]{2,0,1:T(8,128)(2,1)} %copy.77), channel_id=1, source_target_pairs={{28,0},{0,4},{4,8},{8,12},{12,16},{16,20},{20,24},{24,28},{29,1},{... | collective-permute-start | bytes 3145736 | tf_op jit(solution)/shard_map/while/body/eval_jaxpr/ppermute | solution.py:16
  147.4 15.4 %collective-permute-start = (bf16[256,2,1024]{2,0,1:T(8,128)(2,1)}, bf16[256,2,1024]{2,0,1:T(8,128)(2,1)}, u32[]{:S(2)}, u32[]{:S(2)}) collective-permute-start(bf16[256,2,1024]{2,0,1:T(8,128)(2,1)} %copy.77), channel_id=1, source_target_pairs={{28,0},{0,4},{4,8},{8,12},{12,16},{16,20},{20,24},{24,28},{29,1},{... | collective-permute-start | bytes 3145736 | tf_op jit(solution)/shard_map/while/body/eval_jaxpr/ppermute | solution.py:16
  165.1 15.4 %collective-permute-start = (bf16[256,2,1024]{2,0,1:T(8,128)(2,1)}, bf16[256,2,1024]{2,0,1:T(8,128)(2,1)}, u32[]{:S(2)}, u32[]{:S(2)}) collective-permute-start(bf16[256,2,1024]{2,0,1:T(8,128)(2,1)} %copy.77), channel_id=1, source_target_pairs={{28,0},{0,4},{4,8},{8,12},{12,16},{16,20},{20,24},{24,28},{29,1},{... | collective-permute-start | bytes 3145736 | tf_op jit(solution)/shard_map/while/body/eval_jaxpr/ppermute | solution.py:16
  182.8 15.4 %collective-permute-start = (bf16[256,2,1024]{2,0,1:T(8,128)(2,1)}, bf16[256,2,1024]{2,0,1:T(8,128)(2,1)}, u32[]{:S(2)}, u32[]{:S(2)}) collective-permute-start(bf16[256,2,1024]{2,0,1:T(8,128)(2,1)} %copy.77), channel_id=1, source_target_pairs={{28,0},{0,4},{4,8},{8,12},{12,16},{16,20},{20,24},{24,28},{29,1},{... | collective-permute-start | bytes 3145736 | tf_op jit(solution)/shard_map/while/body/eval_jaxpr/ppermute | solution.py:16
  200.5 15.4 %collective-permute-start = (bf16[256,2,1024]{2,0,1:T(8,128)(2,1)}, bf16[256,2,1024]{2,0,1:T(8,128)(2,1)}, u32[]{:S(2)}, u32[]{:S(2)}) collective-permute-start(bf16[256,2,1024]{2,0,1:T(8,128)(2,1)} %copy.77), channel_id=1, source_target_pairs={{28,0},{0,4},{4,8},{8,12},{12,16},{16,20},{20,24},{24,28},{29,1},{... | collective-permute-start | bytes 3145736 | tf_op jit(solution)/shard_map/while/body/eval_jaxpr/ppermute | solution.py:16
  215.9 5.1 %copy-start = (f32[8,2,1536]{2,1,0:T(2,128)}, f32[8,2,1536]{2,1,0:T(2,128)S(1)}, u32[]{:S(2)}) copy-start(f32[8,2,1536]{2,1,0:T(2,128)S(1)} %get-tuple-element.214) | copy-start | bytes 294916
where the time goes:
time: 223 us; the launch traced here: 222 us
  local copies, waits for them, and re-layouts  73.5 us (33%)
  waiting for transfers between devices  58.2 us (26%)
  matrix products  41.5 us (19%)
  other arithmetic  37.8 us (17%)
  starting transfers between devices  10.1 us (5%)
    ppermute x7, waiting for transfers between devices, shifted(): return lax.ppermute(block, axis, route)  38.5 us
    dot_general x8, matrix products, window_samples(): jnp.einsum('ms,qcs->cmq', cross_rows, window_rows, preferred_element_type...  37.1 us
    another operation x7, local copies, waits for them, and re-layouts  15.8 us
    unnamed x8, local copies, waits for them, and re-layouts  14.6 us
    convert_element_type x10, other arithmetic, block_table(): sine = (jnp.sin(angles) * factor).astype(jnp.bfloat16)  13.1 us
    neg x10, other arithmetic, block_table(): imag_rows = jnp.stack([-sine, cosine], axis=1)  11.1 us
    all_to_all x1, local copies, waits for them, and re-layouts, per_device(): lax.all_to_all(columns, 'wide', split_axis=2, concat_axis=0, tiled=True)  10.4 us
    dynamic_slice x14, local copies, waits for them, and re-layouts, slab_samples(): window_gain = lax.dynamic_index_in_dim(x_weight[0], slab_index, 0, False)  10.3 us
  transfers between devices with their start and end apart: 9, of which 9 were waited for; matrix products, arithmetic and copies ran while one was open for 36% of the time, Pallas kernels for 0%

commit v1 on v0

--- a/solution.py
+++ b/solution.py
@@ -66,7 +66,20 @@
         "oqcy,xykc->xoqk", line_table, unpacked, preferred_element_type=jnp.float32
     )
     columns = product.astype(jnp.bfloat16).reshape(item_count, 2, G * band_depth)
-    slab_lines = lax.all_to_all(columns, "wide", split_axis=2, concat_axis=0, tiled=True)
+
+    def extend_the_block(my_data):
+        formed = jnp.concatenate(
+            jax.lax.all_to_all(
+                jnp.stack(jnp.split(my_data, jax.lax.axis_size("wide"), axis=2), axis=0),
+                "wide",
+                0,
+                0,
+            ),
+            axis=0,
+        )
+        return formed
+
+    slab_lines = extend_the_block(columns)
 
     def transform_rows(table_rows, source):
         product = jnp.einsum(

time: 223 us -> 204 us (0.915)
  local copies, waits for them, and re-layouts: 73.5 us -> 54.1 us
    reshape x1 -> x0, local copies, waits for them, and re-layouts: 10.1 us -> none  [per_device(): product.astype(jnp.bfloat16).reshape(item_count, 2, G * band_depth)]
    all_to_all x1, local copies, waits for them, and re-layouts: 10.4 us -> 1.07 us  [extend_the_block(): jax.lax.all_to_all(jnp.stack(jnp.split(my_data, jax.lax.axis_size('wide')...]
    another operation x7 -> x17, local copies, waits for them, and re-layouts: 15.8 us -> 23.5 us
    unnamed x8 -> x13, local copies, waits for them, and re-layouts: 14.6 us -> 6.92 us
  transfers between devices with their start and end apart: 9 -> 9, of which waited for: 9 -> 9; matrix products, arithmetic and copies ran while one was open for 36% -> 39% of each run, Pallas kernels for 0% -> 0%
where the time goes in v1:
time: 204 us; the launch traced here: 202 us
  waiting for transfers between devices  57.7 us (28%)
  local copies, waits for them, and re-layouts  54.1 us (27%)
  matrix products  41.5 us (20%)
  other arithmetic  38.3 us (19%)
  starting transfers between devices  10.1 us (5%)
    ppermute x7, waiting for transfers between devices, shifted(): return lax.ppermute(block, axis, route)  38 us
    dot_general x8, matrix products, window_samples(): jnp.einsum('ms,qcs->cmq', cross_rows, window_rows, preferred_element_type...  37.1 us
    another operation x7, local copies, waits for them, and re-layouts  15.9 us
    convert_element_type x10, other arithmetic, block_table(): sine = (jnp.sin(angles) * factor).astype(jnp.bfloat16)  13.1 us
    neg x10, other arithmetic, block_table(): imag_rows = jnp.stack([-sine, cosine], axis=1)  11.1 us
    dynamic_slice x14, local copies, waits for them, and re-layouts, slab_samples(): window_gain = lax.dynamic_index_in_dim(x_weight[0], slab_index, 0, False)  10.3 us
    all_to_all x1, waiting for transfers between devices, extend_the_block(): jax.lax.all_to_all(jnp.stack(jnp.split(my_data, jax.lax.axis_size('wide')...  10 us
    all_to_all x1, waiting for transfers between devices, per_device(): lax.all_to_all(band_data, 'narrow', split_axis=2, concat_axis=1, tiled=True)  9.64 us
  transfers between devices with their start and end apart: 9, of which 9 were waited for; matrix products, arithmetic and copies ran while one was open for 39% of the time, Pallas kernels for 0%

profile of v1, /device:TPU:0, one launch (start us, length us, event | category | flops | bytes accessed | tf_op | source)
XLA Modules:
  0.0 202.3 jit_solution(1386031301162541681)
XLA Ops:
  3.5 2.5 %fusion.34 = bf16[32,64,64,2]{2,1,3,0:T(8,128)(2,1)S(1)} fusion(bf16[1,64,2,256]{3,1,2,0:T(8,128)(2,1)S(1)} %get-tuple-element.277, bf16[1,64,2,256]{3,1,2,0:T(8,128)(2,1)S(1)} %get-tuple-element.276, bf16[2,32,64,256]{3,2,1,0:T(8,128)(2,1)} %param.7, f32[256]{0:T(256)S(1)} %bitcast.166, f32[64]{0:T(128)S(1)} %fusion.67, f32[32]{0:T(128)S(1)} %fusion.66), kind=kOutput, calls=%fused_computation.44 | convolution fusion | flops 274202624 | bytes 2753920 | tf_op jit(solution)/shard_map/okcz,cxyz->xyko/dot_general | solution.py:56
  9.3 6.3 %all-to-all-start = ((bf16[4,2,32768]{2,1,0:T(2,128)(2,1)}), bf16[4,2,32768]{2,1,0:T(2,128)(2,1)S(1)}, u32[]{:S(2)}, u32[]{:S(2)}) async-start(bf16[4,2,32768]{2,1,0:T(2,128)(2,1)} %reshape.798), calls=%async_computation | async-start | bytes 1048576 | tf_op jit(solution)/shard_map/all_to_all | solution.py:61
  17.8 2.5 %multiply_convert_fusion.3 = (bf16[512,1,256]{2,0,1:T(8,128)(2,1)S(1)}, bf16[512,1,256]{2,0,1:T(8,128)(2,1)S(1)}) fusion(s32[256]{0:T(256)S(1)} %get-tuple-element.288, s32[512]{0:T(512)S(1)} %iota_add_fusion.2), kind=kLoop, calls=%fused_computation.74 | loop fusion | flops 2359296 | bytes 527360 | tf_op jit(solution)/shard_map/convert_element_type | solution.py:26
  20.5 9.6 %all-to-all-done = bf16[4,2,32768]{2,1,0:T(2,128)(2,1)S(1)} async-done(((bf16[4,2,32768]{2,1,0:T(2,128)(2,1)}), bf16[4,2,32768]{2,1,0:T(2,128)(2,1)S(1)}, u32[]{:S(2)}, u32[]{:S(2)}) %all-to-all-start) | async-done | bytes 524320 | tf_op jit(solution)/shard_map/all_to_all | solution.py:61
  35.0 5.1 %copy.33 = bf16[32,2,512,16]{0,3,2,1:T(8,128)(2,1)} copy(bf16[32,2,512,16]{2,3,1,0:T(8,128)(2,1)S(1)} %fusion.37) | data formatting | bytes 2097152 | tf_op jit(solution)/shard_map/convert_element_type | solution.py:68
  40.0 3.4 %slice_bitcast_fusion = (bf16[1,32,2,1024]{1,3,2,0:T(8,128)(2,1)S(1)}, bf16[1,32,2,1024]{1,3,2,0:T(8,128)(2,1)S(1)}, bf16[1,32,2,1024]{1,3,2,0:T(8,128)(2,1)S(1)...) fusion(bf16[32,2,8192]{0,2,1:T(8,128)(2,1)} %bitcast.161), kind=kLoop, calls=%fused_computation.60 | loop fusion | bytes 2097152 | tf_op jit(solution)/shard_map/stack | solution.py:73
  52.4 3.7 %all-to-all-start.1 = ((bf16[8,32,2,1024]{3,1,2,0:T(8,128)(2,1)}), bf16[8,32,2,1024]{3,1,2,0:T(8,128)(2,1)S(1)}, u32[]{:S(2)}, u32[]{:S(2)}) async-start(bf16[8,32,2,1024]{3,1,2,0:T(8,128)(2,1)} %constant_dynamic-update-slice_fusion), calls=%async_computation.1 | async-start | bytes 2097152 | tf_op jit(solution)/shard_map/all_to_all | solution.py:72
  61.4 10.0 %all-to-all-done.1 = bf16[8,32,2,1024]{3,1,2,0:T(8,128)(2,1)S(1)} async-done(((bf16[8,32,2,1024]{3,1,2,0:T(8,128)(2,1)}), bf16[8,32,2,1024]{3,1,2,0:T(8,128)(2,1)S(1)}, u32[]{:S(2)}, u32[]{:S(2)}) %all-to-all-start.1) | async-done | bytes 1048608 | tf_op jit(solution)/shard_map/all_to_all | solution.py:72
  72.6 124.0 %while.18 = (s32[]{:T(128)}, bf16[256,2,1024]{2,0,1:T(8,128)(2,1)}, f32[8,2,1536]{2,1,0:T(2,128)S(1)}, s32[]{:T(128)}, s32[1,8]{1,0:T(1,128)S(1)}, /*index=5*/bf...) while((s32[]{:T(128)}, bf16[256,2,1024]{2,0,1:T(8,128)(2,1)}, ...), condition=%wide.region_2.3_spmd, body=%wide.region_0.2_spmd.sunk | while | flops 2152920576 | bytes 19441996 | solution.py:111
  80.3 4.6 %fusion.88 = f32[2,1536]{1,0:T(2,128)S(1)} fusion(f32[1536,256]{0,1:T(8,128)S(1)} %bitcast_convert_fusion.7, bf16[1,8,1536,1024]{3,2,1,0:T(8,128)(2,1)} %get-tuple-element.371, s32[]{:T(128)S(6)} %select_n.233, bf16[256,2,1024]{2,0,1:T(8,128)(2,1)} %copy.84, bf16[1,256,2,256]{3,1,2,0:T(8,128)(2,1)S(1)} %get-tuple-element.342, ...), kind=kOutput, calls=%fused_computation.5.clone.1 | convolution fusion | flops 2149839872 | bytes 6303748 | tf_op jit(solution)/shard_map/while/body/eval_jaxpr/ms,qcs->cmq/dot_general | solution.py:33
  84.9 5.4 %collective-permute-done = bf16[256,2,1024]{2,0,1:T(8,128)(2,1)} collective-permute-done((bf16[256,2,1024]{2,0,1:T(8,128)(2,1)}, bf16[256,2,1024]{2,0,1:T(8,128)(2,1)}, u32[]{:S(2)}, u32[]{:S(2)}) %collective-permute-start) | collective-permute-done | bytes 1048608 | tf_op jit(solution)/shard_map/while/body/eval_jaxpr/ppermute | solution.py:16
  98.0 4.6 %fusion.88 = f32[2,1536]{1,0:T(2,128)S(1)} fusion(f32[1536,256]{0,1:T(8,128)S(1)} %bitcast_convert_fusion.7, bf16[1,8,1536,1024]{3,2,1,0:T(8,128)(2,1)} %get-tuple-element.371, s32[]{:T(128)S(6)} %select_n.233, bf16[256,2,1024]{2,0,1:T(8,128)(2,1)} %copy.84, bf16[1,256,2,256]{3,1,2,0:T(8,128)(2,1)S(1)} %get-tuple-element.342, ...), kind=kOutput, calls=%fused_computation.5.clone.1 | convolution fusion | flops 2149839872 | bytes 6303748 | tf_op jit(solution)/shard_map/while/body/eval_jaxpr/ms,qcs->cmq/dot_general | solution.py:33
  102.6 5.4 %collective-permute-done = bf16[256,2,1024]{2,0,1:T(8,128)(2,1)} collective-permute-done((bf16[256,2,1024]{2,0,1:T(8,128)(2,1)}, bf16[256,2,1024]{2,0,1:T(8,128)(2,1)}, u32[]{:S(2)}, u32[]{:S(2)}) %collective-permute-start) | collective-permute-done | bytes 1048608 | tf_op jit(solution)/shard_map/while/body/eval_jaxpr/ppermute | solution.py:16
  115.7 4.6 %fusion.88 = f32[2,1536]{1,0:T(2,128)S(1)} fusion(f32[1536,256]{0,1:T(8,128)S(1)} %bitcast_convert_fusion.7, bf16[1,8,1536,1024]{3,2,1,0:T(8,128)(2,1)} %get-tuple-element.371, s32[]{:T(128)S(6)} %select_n.233, bf16[256,2,1024]{2,0,1:T(8,128)(2,1)} %copy.84, bf16[1,256,2,256]{3,1,2,0:T(8,128)(2,1)S(1)} %get-tuple-element.342, ...), kind=kOutput, calls=%fused_computation.5.clone.1 | convolution fusion | flops 2149839872 | bytes 6303748 | tf_op jit(solution)/shard_map/while/body/eval_jaxpr/ms,qcs->cmq/dot_general | solution.py:33
  120.3 5.4 %collective-permute-done = bf16[256,2,1024]{2,0,1:T(8,128)(2,1)} collective-permute-done((bf16[256,2,1024]{2,0,1:T(8,128)(2,1)}, bf16[256,2,1024]{2,0,1:T(8,128)(2,1)}, u32[]{:S(2)}, u32[]{:S(2)}) %collective-permute-start) | collective-permute-done | bytes 1048608 | tf_op jit(solution)/shard_map/while/body/eval_jaxpr/ppermute | solution.py:16
  133.4 4.6 %fusion.88 = f32[2,1536]{1,0:T(2,128)S(1)} fusion(f32[1536,256]{0,1:T(8,128)S(1)} %bitcast_convert_fusion.7, bf16[1,8,1536,1024]{3,2,1,0:T(8,128)(2,1)} %get-tuple-element.371, s32[]{:T(128)S(6)} %select_n.233, bf16[256,2,1024]{2,0,1:T(8,128)(2,1)} %copy.84, bf16[1,256,2,256]{3,1,2,0:T(8,128)(2,1)S(1)} %get-tuple-element.342, ...), kind=kOutput, calls=%fused_computation.5.clone.1 | convolution fusion | flops 2149839872 | bytes 6303748 | tf_op jit(solution)/shard_map/while/body/eval_jaxpr/ms,qcs->cmq/dot_general | solution.py:33
  138.0 5.4 %collective-permute-done = bf16[256,2,1024]{2,0,1:T(8,128)(2,1)} collective-permute-done((bf16[256,2,1024]{2,0,1:T(8,128)(2,1)}, bf16[256,2,1024]{2,0,1:T(8,128)(2,1)}, u32[]{:S(2)}, u32[]{:S(2)}) %collective-permute-start) | collective-permute-done | bytes 1048608 | tf_op jit(solution)/shard_map/while/body/eval_jaxpr/ppermute | solution.py:16
  151.1 4.6 %fusion.88 = f32[2,1536]{1,0:T(2,128)S(1)} fusion(f32[1536,256]{0,1:T(8,128)S(1)} %bitcast_convert_fusion.7, bf16[1,8,1536,1024]{3,2,1,0:T(8,128)(2,1)} %get-tuple-element.371, s32[]{:T(128)S(6)} %select_n.233, bf16[256,2,1024]{2,0,1:T(8,128)(2,1)} %copy.84, bf16[1,256,2,256]{3,1,2,0:T(8,128)(2,1)S(1)} %get-tuple-element.342, ...), kind=kOutput, calls=%fused_computation.5.clone.1 | convolution fusion | flops 2149839872 | bytes 6303748 | tf_op jit(solution)/shard_map/while/body/eval_jaxpr/ms,qcs->cmq/dot_general | solution.py:33
  155.7 5.4 %collective-permute-done = bf16[256,2,1024]{2,0,1:T(8,128)(2,1)} collective-permute-done((bf16[256,2,1024]{2,0,1:T(8,128)(2,1)}, bf16[256,2,1024]{2,0,1:T(8,128)(2,1)}, u32[]{:S(2)}, u32[]{:S(2)}) %collective-permute-start) | collective-permute-done | bytes 1048608 | tf_op jit(solution)/shard_map/while/body/eval_jaxpr/ppermute | solution.py:16
  168.8 4.6 %fusion.88 = f32[2,1536]{1,0:T(2,128)S(1)} fusion(f32[1536,256]{0,1:T(8,128)S(1)} %bitcast_convert_fusion.7, bf16[1,8,1536,1024]{3,2,1,0:T(8,128)(2,1)} %get-tuple-element.371, s32[]{:T(128)S(6)} %select_n.233, bf16[256,2,1024]{2,0,1:T(8,128)(2,1)} %copy.84, bf16[1,256,2,256]{3,1,2,0:T(8,128)(2,1)S(1)} %get-tuple-element.342, ...), kind=kOutput, calls=%fused_computation.5.clone.1 | convolution fusion | flops 2149839872 | bytes 6303748 | tf_op jit(solution)/shard_map/while/body/eval_jaxpr/ms,qcs->cmq/dot_general | solution.py:33
  173.4 5.4 %collective-permute-done = bf16[256,2,1024]{2,0,1:T(8,128)(2,1)} collective-permute-done((bf16[256,2,1024]{2,0,1:T(8,128)(2,1)}, bf16[256,2,1024]{2,0,1:T(8,128)(2,1)}, u32[]{:S(2)}, u32[]{:S(2)}) %collective-permute-start) | collective-permute-done | bytes 1048608 | tf_op jit(solution)/shard_map/while/body/eval_jaxpr/ppermute | solution.py:16
  186.5 4.6 %fusion.88 = f32[2,1536]{1,0:T(2,128)S(1)} fusion(f32[1536,256]{0,1:T(8,128)S(1)} %bitcast_convert_fusion.7, bf16[1,8,1536,1024]{3,2,1,0:T(8,128)(2,1)} %get-tuple-element.371, s32[]{:T(128)S(6)} %select_n.233, bf16[256,2,1024]{2,0,1:T(8,128)(2,1)} %copy.84, bf16[1,256,2,256]{3,1,2,0:T(8,128)(2,1)S(1)} %get-tuple-element.342, ...), kind=kOutput, calls=%fused_computation.5.clone.1 | convolution fusion | flops 2149839872 | bytes 6303748 | tf_op jit(solution)/shard_map/while/body/eval_jaxpr/ms,qcs->cmq/dot_general | solution.py:33
  191.1 5.4 %collective-permute-done = bf16[256,2,1024]{2,0,1:T(8,128)(2,1)} collective-permute-done((bf16[256,2,1024]{2,0,1:T(8,128)(2,1)}, bf16[256,2,1024]{2,0,1:T(8,128)(2,1)}, u32[]{:S(2)}, u32[]{:S(2)}) %collective-permute-start) | collective-permute-done | bytes 1048608 | tf_op jit(solution)/shard_map/while/body/eval_jaxpr/ppermute | solution.py:16
  196.5 5.1 %fusion.29 = f32[2,1536]{1,0:T(2,128)S(1)} fusion(f32[1536,256]{0,1:T(8,128)} %copy.46, bf16[1,8,1536,1024]{3,2,1,0:T(8,128)(2,1)} %get-tuple-element.381, s32[]{:T(128)S(6)} %select_n.180, bf16[256,2,1024]{2,0,1:T(8,128)(2,1)} %get-tuple-element.215, bf16[1,256,2,256]{3,1,2,0:T(8,128)(2,1)S(1)} %get-tuple-element.275, ...), kind=kOutput, calls=%fused_computation.43 | convolution fusion | flops 2150626304 | bytes 6303748 | tf_op jit(solution)/shard_map/ms,qcs->cmq/dot_general | solution.py:33
  (123 shorter events, 83.2 us)
Async XLA Ops:
  9.3 20.8 %all-to-all-start = ((bf16[4,2,32768]{2,1,0:T(2,128)(2,1)}), bf16[4,2,32768]{2,1,0:T(2,128)(2,1)S(1)}, u32[]{:S(2)}, u32[]{:S(2)}) async-start(bf16[4,2,32768]{2,1,0:T(2,128)(2,1)} %reshape.798), calls=%async_computation | async-start | bytes 1048576 | tf_op jit(solution)/shard_map/all_to_all | solution.py:61
  52.4 19.1 %all-to-all-start.1 = ((bf16[8,32,2,1024]{3,1,2,0:T(8,128)(2,1)}), bf16[8,32,2,1024]{3,1,2,0:T(8,128)(2,1)S(1)}, u32[]{:S(2)}, u32[]{:S(2)}) async-start(bf16[8,32,2,1024]{3,1,2,0:T(8,128)(2,1)} %constant_dynamic-update-slice_fusion), calls=%async_computation.1 | async-start | bytes 2097152 | tf_op jit(solution)/shard_map/all_to_all | solution.py:72
  57.4 15.2 %copy-start.1 = (s32[1,8]{1,0:T(1,128)S(1)}, s32[1,8]{1,0:T(1,128)}, u32[]{:S(2)}) copy-start(s32[1,8]{1,0:T(1,128)} %param.9) | copy-start | bytes 100
  74.8 15.4 %collective-permute-start = (bf16[256,2,1024]{2,0,1:T(8,128)(2,1)}, bf16[256,2,1024]{2,0,1:T(8,128)(2,1)}, u32[]{:S(2)}, u32[]{:S(2)}) collective-permute-start(bf16[256,2,1024]{2,0,1:T(8,128)(2,1)} %copy.84), channel_id=1, source_target_pairs={{28,0},{0,4},{4,8},{8,12},{12,16},{16,20},{20,24},{24,28},{29,1},{... | collective-permute-start | bytes 3145736 | tf_op jit(solution)/shard_map/while/body/eval_jaxpr/ppermute | solution.py:16
  92.6 15.4 %collective-permute-start = (bf16[256,2,1024]{2,0,1:T(8,128)(2,1)}, bf16[256,2,1024]{2,0,1:T(8,128)(2,1)}, u32[]{:S(2)}, u32[]{:S(2)}) collective-permute-start(bf16[256,2,1024]{2,0,1:T(8,128)(2,1)} %copy.84), channel_id=1, source_target_pairs={{28,0},{0,4},{4,8},{8,12},{12,16},{16,20},{20,24},{24,28},{29,1},{... | collective-permute-start | bytes 3145736 | tf_op jit(solution)/shard_map/while/body/eval_jaxpr/ppermute | solution.py:16
  110.3 15.4 %collective-permute-start = (bf16[256,2,1024]{2,0,1:T(8,128)(2,1)}, bf16[256,2,1024]{2,0,1:T(8,128)(2,1)}, u32[]{:S(2)}, u32[]{:S(2)}) collective-permute-start(bf16[256,2,1024]{2,0,1:T(8,128)(2,1)} %copy.84), channel_id=1, source_target_pairs={{28,0},{0,4},{4,8},{8,12},{12,16},{16,20},{20,24},{24,28},{29,1},{... | collective-permute-start | bytes 3145736 | tf_op jit(solution)/shard_map/while/body/eval_jaxpr/ppermute | solution.py:16
  128.0 15.4 %collective-permute-start = (bf16[256,2,1024]{2,0,1:T(8,128)(2,1)}, bf16[256,2,1024]{2,0,1:T(8,128)(2,1)}, u32[]{:S(2)}, u32[]{:S(2)}) collective-permute-start(bf16[256,2,1024]{2,0,1:T(8,128)(2,1)} %copy.84), channel_id=1, source_target_pairs={{28,0},{0,4},{4,8},{8,12},{12,16},{16,20},{20,24},{24,28},{29,1},{... | collective-permute-start | bytes 3145736 | tf_op jit(solution)/shard_map/while/body/eval_jaxpr/ppermute | solution.py:16
  145.7 15.4 %collective-permute-start = (bf16[256,2,1024]{2,0,1:T(8,128)(2,1)}, bf16[256,2,1024]{2,0,1:T(8,128)(2,1)}, u32[]{:S(2)}, u32[]{:S(2)}) collective-permute-start(bf16[256,2,1024]{2,0,1:T(8,128)(2,1)} %copy.84), channel_id=1, source_target_pairs={{28,0},{0,4},{4,8},{8,12},{12,16},{16,20},{20,24},{24,28},{29,1},{... | collective-permute-start | bytes 3145736 | tf_op jit(solution)/shard_map/while/body/eval_jaxpr/ppermute | solution.py:16
  163.4 15.4 %collective-permute-start = (bf16[256,2,1024]{2,0,1:T(8,128)(2,1)}, bf16[256,2,1024]{2,0,1:T(8,128)(2,1)}, u32[]{:S(2)}, u32[]{:S(2)}) collective-permute-start(bf16[256,2,1024]{2,0,1:T(8,128)(2,1)} %copy.84), channel_id=1, source_target_pairs={{28,0},{0,4},{4,8},{8,12},{12,16},{16,20},{20,24},{24,28},{29,1},{... | collective-permute-start | bytes 3145736 | tf_op jit(solution)/shard_map/while/body/eval_jaxpr/ppermute | solution.py:16
  181.1 15.4 %collective-permute-start = (bf16[256,2,1024]{2,0,1:T(8,128)(2,1)}, bf16[256,2,1024]{2,0,1:T(8,128)(2,1)}, u32[]{:S(2)}, u32[]{:S(2)}) collective-permute-start(bf16[256,2,1024]{2,0,1:T(8,128)(2,1)} %copy.84), channel_id=1, source_target_pairs={{28,0},{0,4},{4,8},{8,12},{12,16},{16,20},{20,24},{24,28},{29,1},{... | collective-permute-start | bytes 3145736 | tf_op jit(solution)/shard_map/while/body/eval_jaxpr/ppermute | solution.py:16
  196.5 5.1 %copy-start = (f32[8,2,1536]{2,1,0:T(2,128)}, f32[8,2,1536]{2,1,0:T(2,128)S(1)}, u32[]{:S(2)}) copy-start(f32[8,2,1536]{2,1,0:T(2,128)S(1)} %get-tuple-element.214) | copy-start | bytes 294916
